TPU v7x, 32 devices: a whole 2x2x4 slice. The times are simulated.
32 devices in a mesh: prow: 4 (over y, core), pcol: 8 (over z, x).
Axes of the slice: x: 2, y: 2, z: 4, core: 2. Of those that a mesh axis runs over, the one named last changes fastest.
Arguments:
- inverse_cov: bfloat16 [8192, 8192], P('prow', 'pcol'), may hold values from -0.5 to 4.5, as said below
- cosines: float32 [8192, 8192], P('prow', 'pcol'), may hold values from -1 to 1, as said below
- sky_maps: bfloat16 [8192, 192], P('pcol'), may hold values from -6 to 6
Outputs:
- filtered: bfloat16 [8192, 192], P('prow')
- spectra: float32 [64, 192], replicated
Inputs may be any that keep to these rules, and one draw needn't show every extreme that they name: `inverse_cov`: symmetric, with a dominant diagonal. `cosines`: symmetric.
All inputs are finite; a program needn't handle non-finite values.
Results may differ from a plain program's by a relative error of at most 0.0033.
Values may be sent and summed in bfloat16 or wider, within the bound.
A program may use at most 128 MiB of HBM per device.

v0:
```python
import jax
import jax.numpy as jnp
from jax import lax
from jax.sharding import PartitionSpec as P

NPIX = 8192
L = 64
LMIN = 2
GROUP = 4


def next_legendre(previous, current, cosine, degree):
    return ((2.0 * degree - 1.0) * cosine * current - (degree - 1.0) * previous) / degree


def per_device(inverse_cov, cosines, sky_maps):
    cols_here = inverse_cov.shape[1]
    partial_value = jnp.dot(inverse_cov, sky_maps, preferred_element_type=jnp.float32)
    filtered = lax.psum(partial_value, "pcol").astype(jnp.bfloat16)
    column_index = lax.axis_index("pcol")
    full_maps = lax.all_gather(filtered, "prow", axis=0, tiled=True)
    filtered_cols = lax.dynamic_slice_in_dim(full_maps, column_index * cols_here, cols_here, 0)
    rows_f32 = filtered.astype(jnp.float32)
    previous = jnp.ones_like(cosines)
    current = cosines

    def advance(carried, turn_index):
        previous, current = carried
        term_list = []
        weights = []
        for offset in range(GROUP):
            degree = (LMIN + turn_index * GROUP + offset).astype(jnp.float32)
            next_term = next_legendre(previous, current, cosines, degree)
            term_list.append(next_term.astype(jnp.bfloat16))
            weights.append((2.0 * degree + 1.0) / NPIX)
            previous, current = (current, next_term)
        stacked = jnp.stack(term_list)
        product = jnp.einsum(
            "grc,cm->grm", stacked, filtered_cols, preferred_element_type=jnp.float32
        )
        quadratic = jnp.sum(product * rows_f32[None], axis=1)
        return ((previous, current), quadratic * jnp.stack(weights)[:, None])

    carried, partial_spectra = lax.scan(
        advance, (previous, current), jnp.arange(L // GROUP, dtype=jnp.int32)
    )
    spectra = lax.psum(partial_spectra.reshape(L, -1), ("prow", "pcol"))
    return (filtered, spectra)


def solution(mesh):
    in_specs = (P("prow", "pcol"), P("prow", "pcol"), P("pcol", None))
    out_specs = (P("prow", None), P())
    return jax.shard_map(
        per_device, mesh=mesh, in_specs=in_specs, out_specs=out_specs, check_vma=False
    )
```

profile of v0, /device:TPU:0, one launch (start us, length us, event | category | flops | bytes accessed | tf_op | source)
XLA Modules:
  0.0 855.3 jit_solution(4507010402875812031)
XLA Ops:
  11.9 82.8 %all-reduce.1 = bf16[2048,192]{0,1:T(8,128)(2,1)} all-reduce(f32[2048,192]{0,1:T(8,128)S(1)} %fusion.15), channel_id=1, replica_groups=mesh['prow'=4,'pcol'=8] {'pcol'}, use_global_device_ids=true, to_apply=%region_0.0 | all-reduce | flops 393216 | bytes 2359296 | tf_op jit(solution)/shard_map/psum | solution.py:19
  97.2 8.5 copy.9
  105.7 16.7 %all-gather.2.cloned.1.call-done = bf16[8192,192]{0,1:T(8,128)(2,1)} async-done(((bf16[2048,192]{0,1:T(8,128)(2,1)}), bf16[8192,192]{0,1:T(8,128)(2,1)}) %all-gather.2.cloned.1.call-update) | async-done | bytes 3145744 | tf_op jit(solution)/shard_map/all_gather | solution.py:21
  123.5 684.9 %while.18 = (s32[]{:T(128)}, f32[2048,1024]{1,0:T(8,128)}, f32[2048,1024]{1,0:T(8,128)}, f32[16,4,192]{2,1,0:T(4,128)S(1)}, s32[16]{0:T(128)S(1)}, /*index=5*/f3...) while((s32[]{:T(128)}, f32[2048,1024]{1,0:T(8,128)}, ...), condition=%wide.region_3.4_spmd.clone, body=%wide.region_1.3_spmd.clone.sunk | while | flops 3325034496 | bytes 194916608 | solution.py:44
  124.8 10.9 %convert_bitcast_fusion.6 = (bf16[1,2048,1024]{2,1,0:T(8,128)(2,1)S(1)}, f32[2048,1024]{1,0:T(8,128)S(1)}, bf16[1,2048,1024]{2,1,0:T(8,128)(2,1)}) fusion(f32[]{:T(128)} %bitcast.41, f32[]{:T(128)S(6)} %sub.98, f32[]{:T(128)} %bitcast.42, f32[2048,1024]{1,0:T(8,128)} %get-tuple-element.271, f32[]{:T(128)S(6)} %sub.99, f32[]{:T(128)} %bitcast.43, ...), kind=kLoop, calls=%fused_computation.16.clone.1 | loop fusion | flops 37748736 | bytes 41943076 | tf_op jit(solution)/shard_map/while/body/eval_jaxpr/stack | solution.py:37
  135.7 11.3 %convert_bitcast_fusion.7 = (bf16[1,2048,1024]{2,1,0:T(8,128)(2,1)}, f32[2048,1024]{1,0:T(8,128)}, bf16[1,2048,1024]{2,1,0:T(8,128)(2,1)}) fusion(f32[]{:T(128)} %bitcast.44, f32[]{:T(128)} %bitcast.42, f32[2048,1024]{1,0:T(8,128)} %get-tuple-element.271, f32[]{:T(128)S(6)} %sub.99, f32[]{:T(128)} %bitcast.43, f32[2048,1024]{1,0:T(8,128)} %get-tuple-element.270, ...), kind=kLoop, calls=%fused_computation.15.clone.1 | loop fusion | flops 37748736 | bytes 50331684 | tf_op jit(solution)/shard_map/while/body/eval_jaxpr/stack | solution.py:37
  153.5 7.9 multiply_reduce_fusion.2
  162.9 12.4 %convert_bitcast_fusion.6 = (bf16[1,2048,1024]{2,1,0:T(8,128)(2,1)S(1)}, f32[2048,1024]{1,0:T(8,128)S(1)}, bf16[1,2048,1024]{2,1,0:T(8,128)(2,1)}) fusion(f32[]{:T(128)} %bitcast.41, f32[]{:T(128)S(6)} %sub.98, f32[]{:T(128)} %bitcast.42, f32[2048,1024]{1,0:T(8,128)} %get-tuple-element.271, f32[]{:T(128)S(6)} %sub.99, f32[]{:T(128)} %bitcast.43, ...), kind=kLoop, calls=%fused_computation.16.clone.1 | loop fusion | flops 37748736 | bytes 41943076 | tf_op jit(solution)/shard_map/while/body/eval_jaxpr/stack | solution.py:37
  175.3 14.8 %convert_bitcast_fusion.7 = (bf16[1,2048,1024]{2,1,0:T(8,128)(2,1)}, f32[2048,1024]{1,0:T(8,128)}, bf16[1,2048,1024]{2,1,0:T(8,128)(2,1)}) fusion(f32[]{:T(128)} %bitcast.44, f32[]{:T(128)} %bitcast.42, f32[2048,1024]{1,0:T(8,128)} %get-tuple-element.271, f32[]{:T(128)S(6)} %sub.99, f32[]{:T(128)} %bitcast.43, f32[2048,1024]{1,0:T(8,128)} %get-tuple-element.270, ...), kind=kLoop, calls=%fused_computation.15.clone.1 | loop fusion | flops 37748736 | bytes 50331684 | tf_op jit(solution)/shard_map/while/body/eval_jaxpr/stack | solution.py:37
  196.6 7.9 multiply_reduce_fusion.2
  206.0 12.4 %convert_bitcast_fusion.6 = (bf16[1,2048,1024]{2,1,0:T(8,128)(2,1)S(1)}, f32[2048,1024]{1,0:T(8,128)S(1)}, bf16[1,2048,1024]{2,1,0:T(8,128)(2,1)}) fusion(f32[]{:T(128)} %bitcast.41, f32[]{:T(128)S(6)} %sub.98, f32[]{:T(128)} %bitcast.42, f32[2048,1024]{1,0:T(8,128)} %get-tuple-element.271, f32[]{:T(128)S(6)} %sub.99, f32[]{:T(128)} %bitcast.43, ...), kind=kLoop, calls=%fused_computation.16.clone.1 | loop fusion | flops 37748736 | bytes 41943076 | tf_op jit(solution)/shard_map/while/body/eval_jaxpr/stack | solution.py:37
  218.4 14.8 %convert_bitcast_fusion.7 = (bf16[1,2048,1024]{2,1,0:T(8,128)(2,1)}, f32[2048,1024]{1,0:T(8,128)}, bf16[1,2048,1024]{2,1,0:T(8,128)(2,1)}) fusion(f32[]{:T(128)} %bitcast.44, f32[]{:T(128)} %bitcast.42, f32[2048,1024]{1,0:T(8,128)} %get-tuple-element.271, f32[]{:T(128)S(6)} %sub.99, f32[]{:T(128)} %bitcast.43, f32[2048,1024]{1,0:T(8,128)} %get-tuple-element.270, ...), kind=kLoop, calls=%fused_computation.15.clone.1 | loop fusion | flops 37748736 | bytes 50331684 | tf_op jit(solution)/shard_map/while/body/eval_jaxpr/stack | solution.py:37
  239.7 7.9 multiply_reduce_fusion.2
  249.1 12.4 %convert_bitcast_fusion.6 = (bf16[1,2048,1024]{2,1,0:T(8,128)(2,1)S(1)}, f32[2048,1024]{1,0:T(8,128)S(1)}, bf16[1,2048,1024]{2,1,0:T(8,128)(2,1)}) fusion(f32[]{:T(128)} %bitcast.41, f32[]{:T(128)S(6)} %sub.98, f32[]{:T(128)} %bitcast.42, f32[2048,1024]{1,0:T(8,128)} %get-tuple-element.271, f32[]{:T(128)S(6)} %sub.99, f32[]{:T(128)} %bitcast.43, ...), kind=kLoop, calls=%fused_computation.16.clone.1 | loop fusion | flops 37748736 | bytes 41943076 | tf_op jit(solution)/shard_map/while/body/eval_jaxpr/stack | solution.py:37
  261.5 14.8 %convert_bitcast_fusion.7 = (bf16[1,2048,1024]{2,1,0:T(8,128)(2,1)}, f32[2048,1024]{1,0:T(8,128)}, bf16[1,2048,1024]{2,1,0:T(8,128)(2,1)}) fusion(f32[]{:T(128)} %bitcast.44, f32[]{:T(128)} %bitcast.42, f32[2048,1024]{1,0:T(8,128)} %get-tuple-element.271, f32[]{:T(128)S(6)} %sub.99, f32[]{:T(128)} %bitcast.43, f32[2048,1024]{1,0:T(8,128)} %get-tuple-element.270, ...), kind=kLoop, calls=%fused_computation.15.clone.1 | loop fusion | flops 37748736 | bytes 50331684 | tf_op jit(solution)/shard_map/while/body/eval_jaxpr/stack | solution.py:37
  282.8 7.9 multiply_reduce_fusion.2
  292.2 12.4 %convert_bitcast_fusion.6 = (bf16[1,2048,1024]{2,1,0:T(8,128)(2,1)S(1)}, f32[2048,1024]{1,0:T(8,128)S(1)}, bf16[1,2048,1024]{2,1,0:T(8,128)(2,1)}) fusion(f32[]{:T(128)} %bitcast.41, f32[]{:T(128)S(6)} %sub.98, f32[]{:T(128)} %bitcast.42, f32[2048,1024]{1,0:T(8,128)} %get-tuple-element.271, f32[]{:T(128)S(6)} %sub.99, f32[]{:T(128)} %bitcast.43, ...), kind=kLoop, calls=%fused_computation.16.clone.1 | loop fusion | flops 37748736 | bytes 41943076 | tf_op jit(solution)/shard_map/while/body/eval_jaxpr/stack | solution.py:37
  304.6 14.8 %convert_bitcast_fusion.7 = (bf16[1,2048,1024]{2,1,0:T(8,128)(2,1)}, f32[2048,1024]{1,0:T(8,128)}, bf16[1,2048,1024]{2,1,0:T(8,128)(2,1)}) fusion(f32[]{:T(128)} %bitcast.44, f32[]{:T(128)} %bitcast.42, f32[2048,1024]{1,0:T(8,128)} %get-tuple-element.271, f32[]{:T(128)S(6)} %sub.99, f32[]{:T(128)} %bitcast.43, f32[2048,1024]{1,0:T(8,128)} %get-tuple-element.270, ...), kind=kLoop, calls=%fused_computation.15.clone.1 | loop fusion | flops 37748736 | bytes 50331684 | tf_op jit(solution)/shard_map/while/body/eval_jaxpr/stack | solution.py:37
  326.0 7.9 multiply_reduce_fusion.2
  335.3 12.4 %convert_bitcast_fusion.6 = (bf16[1,2048,1024]{2,1,0:T(8,128)(2,1)S(1)}, f32[2048,1024]{1,0:T(8,128)S(1)}, bf16[1,2048,1024]{2,1,0:T(8,128)(2,1)}) fusion(f32[]{:T(128)} %bitcast.41, f32[]{:T(128)S(6)} %sub.98, f32[]{:T(128)} %bitcast.42, f32[2048,1024]{1,0:T(8,128)} %get-tuple-element.271, f32[]{:T(128)S(6)} %sub.99, f32[]{:T(128)} %bitcast.43, ...), kind=kLoop, calls=%fused_computation.16.clone.1 | loop fusion | flops 37748736 | bytes 41943076 | tf_op jit(solution)/shard_map/while/body/eval_jaxpr/stack | solution.py:37
  347.8 14.8 %convert_bitcast_fusion.7 = (bf16[1,2048,1024]{2,1,0:T(8,128)(2,1)}, f32[2048,1024]{1,0:T(8,128)}, bf16[1,2048,1024]{2,1,0:T(8,128)(2,1)}) fusion(f32[]{:T(128)} %bitcast.44, f32[]{:T(128)} %bitcast.42, f32[2048,1024]{1,0:T(8,128)} %get-tuple-element.271, f32[]{:T(128)S(6)} %sub.99, f32[]{:T(128)} %bitcast.43, f32[2048,1024]{1,0:T(8,128)} %get-tuple-element.270, ...), kind=kLoop, calls=%fused_computation.15.clone.1 | loop fusion | flops 37748736 | bytes 50331684 | tf_op jit(solution)/shard_map/while/body/eval_jaxpr/stack | solution.py:37
  369.1 7.9 multiply_reduce_fusion.2
  378.5 12.4 %convert_bitcast_fusion.6 = (bf16[1,2048,1024]{2,1,0:T(8,128)(2,1)S(1)}, f32[2048,1024]{1,0:T(8,128)S(1)}, bf16[1,2048,1024]{2,1,0:T(8,128)(2,1)}) fusion(f32[]{:T(128)} %bitcast.41, f32[]{:T(128)S(6)} %sub.98, f32[]{:T(128)} %bitcast.42, f32[2048,1024]{1,0:T(8,128)} %get-tuple-element.271, f32[]{:T(128)S(6)} %sub.99, f32[]{:T(128)} %bitcast.43, ...), kind=kLoop, calls=%fused_computation.16.clone.1 | loop fusion | flops 37748736 | bytes 41943076 | tf_op jit(solution)/shard_map/while/body/eval_jaxpr/stack | solution.py:37
  390.9 14.8 %convert_bitcast_fusion.7 = (bf16[1,2048,1024]{2,1,0:T(8,128)(2,1)}, f32[2048,1024]{1,0:T(8,128)}, bf16[1,2048,1024]{2,1,0:T(8,128)(2,1)}) fusion(f32[]{:T(128)} %bitcast.44, f32[]{:T(128)} %bitcast.42, f32[2048,1024]{1,0:T(8,128)} %get-tuple-element.271, f32[]{:T(128)S(6)} %sub.99, f32[]{:T(128)} %bitcast.43, f32[2048,1024]{1,0:T(8,128)} %get-tuple-element.270, ...), kind=kLoop, calls=%fused_computation.15.clone.1 | loop fusion | flops 37748736 | bytes 50331684 | tf_op jit(solution)/shard_map/while/body/eval_jaxpr/stack | solution.py:37
  412.2 7.9 multiply_reduce_fusion.2
  421.6 12.4 %convert_bitcast_fusion.6 = (bf16[1,2048,1024]{2,1,0:T(8,128)(2,1)S(1)}, f32[2048,1024]{1,0:T(8,128)S(1)}, bf16[1,2048,1024]{2,1,0:T(8,128)(2,1)}) fusion(f32[]{:T(128)} %bitcast.41, f32[]{:T(128)S(6)} %sub.98, f32[]{:T(128)} %bitcast.42, f32[2048,1024]{1,0:T(8,128)} %get-tuple-element.271, f32[]{:T(128)S(6)} %sub.99, f32[]{:T(128)} %bitcast.43, ...), kind=kLoop, calls=%fused_computation.16.clone.1 | loop fusion | flops 37748736 | bytes 41943076 | tf_op jit(solution)/shard_map/while/body/eval_jaxpr/stack | solution.py:37
  434.0 14.8 %convert_bitcast_fusion.7 = (bf16[1,2048,1024]{2,1,0:T(8,128)(2,1)}, f32[2048,1024]{1,0:T(8,128)}, bf16[1,2048,1024]{2,1,0:T(8,128)(2,1)}) fusion(f32[]{:T(128)} %bitcast.44, f32[]{:T(128)} %bitcast.42, f32[2048,1024]{1,0:T(8,128)} %get-tuple-element.271, f32[]{:T(128)S(6)} %sub.99, f32[]{:T(128)} %bitcast.43, f32[2048,1024]{1,0:T(8,128)} %get-tuple-element.270, ...), kind=kLoop, calls=%fused_computation.15.clone.1 | loop fusion | flops 37748736 | bytes 50331684 | tf_op jit(solution)/shard_map/while/body/eval_jaxpr/stack | solution.py:37
  455.3 7.9 multiply_reduce_fusion.2
  464.7 12.4 %convert_bitcast_fusion.6 = (bf16[1,2048,1024]{2,1,0:T(8,128)(2,1)S(1)}, f32[2048,1024]{1,0:T(8,128)S(1)}, bf16[1,2048,1024]{2,1,0:T(8,128)(2,1)}) fusion(f32[]{:T(128)} %bitcast.41, f32[]{:T(128)S(6)} %sub.98, f32[]{:T(128)} %bitcast.42, f32[2048,1024]{1,0:T(8,128)} %get-tuple-element.271, f32[]{:T(128)S(6)} %sub.99, f32[]{:T(128)} %bitcast.43, ...), kind=kLoop, calls=%fused_computation.16.clone.1 | loop fusion | flops 37748736 | bytes 41943076 | tf_op jit(solution)/shard_map/while/body/eval_jaxpr/stack | solution.py:37
  477.1 14.8 %convert_bitcast_fusion.7 = (bf16[1,2048,1024]{2,1,0:T(8,128)(2,1)}, f32[2048,1024]{1,0:T(8,128)}, bf16[1,2048,1024]{2,1,0:T(8,128)(2,1)}) fusion(f32[]{:T(128)} %bitcast.44, f32[]{:T(128)} %bitcast.42, f32[2048,1024]{1,0:T(8,128)} %get-tuple-element.271, f32[]{:T(128)S(6)} %sub.99, f32[]{:T(128)} %bitcast.43, f32[2048,1024]{1,0:T(8,128)} %get-tuple-element.270, ...), kind=kLoop, calls=%fused_computation.15.clone.1 | loop fusion | flops 37748736 | bytes 50331684 | tf_op jit(solution)/shard_map/while/body/eval_jaxpr/stack | solution.py:37
  498.4 7.9 multiply_reduce_fusion.2
  507.8 12.4 %convert_bitcast_fusion.6 = (bf16[1,2048,1024]{2,1,0:T(8,128)(2,1)S(1)}, f32[2048,1024]{1,0:T(8,128)S(1)}, bf16[1,2048,1024]{2,1,0:T(8,128)(2,1)}) fusion(f32[]{:T(128)} %bitcast.41, f32[]{:T(128)S(6)} %sub.98, f32[]{:T(128)} %bitcast.42, f32[2048,1024]{1,0:T(8,128)} %get-tuple-element.271, f32[]{:T(128)S(6)} %sub.99, f32[]{:T(128)} %bitcast.43, ...), kind=kLoop, calls=%fused_computation.16.clone.1 | loop fusion | flops 37748736 | bytes 41943076 | tf_op jit(solution)/shard_map/while/body/eval_jaxpr/stack | solution.py:37
  520.2 14.8 %convert_bitcast_fusion.7 = (bf16[1,2048,1024]{2,1,0:T(8,128)(2,1)}, f32[2048,1024]{1,0:T(8,128)}, bf16[1,2048,1024]{2,1,0:T(8,128)(2,1)}) fusion(f32[]{:T(128)} %bitcast.44, f32[]{:T(128)} %bitcast.42, f32[2048,1024]{1,0:T(8,128)} %get-tuple-element.271, f32[]{:T(128)S(6)} %sub.99, f32[]{:T(128)} %bitcast.43, f32[2048,1024]{1,0:T(8,128)} %get-tuple-element.270, ...), kind=kLoop, calls=%fused_computation.15.clone.1 | loop fusion | flops 37748736 | bytes 50331684 | tf_op jit(solution)/shard_map/while/body/eval_jaxpr/stack | solution.py:37
  541.6 7.9 multiply_reduce_fusion.2
  550.9 12.4 %convert_bitcast_fusion.6 = (bf16[1,2048,1024]{2,1,0:T(8,128)(2,1)S(1)}, f32[2048,1024]{1,0:T(8,128)S(1)}, bf16[1,2048,1024]{2,1,0:T(8,128)(2,1)}) fusion(f32[]{:T(128)} %bitcast.41, f32[]{:T(128)S(6)} %sub.98, f32[]{:T(128)} %bitcast.42, f32[2048,1024]{1,0:T(8,128)} %get-tuple-element.271, f32[]{:T(128)S(6)} %sub.99, f32[]{:T(128)} %bitcast.43, ...), kind=kLoop, calls=%fused_computation.16.clone.1 | loop fusion | flops 37748736 | bytes 41943076 | tf_op jit(solution)/shard_map/while/body/eval_jaxpr/stack | solution.py:37
  563.4 14.8 %convert_bitcast_fusion.7 = (bf16[1,2048,1024]{2,1,0:T(8,128)(2,1)}, f32[2048,1024]{1,0:T(8,128)}, bf16[1,2048,1024]{2,1,0:T(8,128)(2,1)}) fusion(f32[]{:T(128)} %bitcast.44, f32[]{:T(128)} %bitcast.42, f32[2048,1024]{1,0:T(8,128)} %get-tuple-element.271, f32[]{:T(128)S(6)} %sub.99, f32[]{:T(128)} %bitcast.43, f32[2048,1024]{1,0:T(8,128)} %get-tuple-element.270, ...), kind=kLoop, calls=%fused_computation.15.clone.1 | loop fusion | flops 37748736 | bytes 50331684 | tf_op jit(solution)/shard_map/while/body/eval_jaxpr/stack | solution.py:37
  584.7 7.9 multiply_reduce_fusion.2
  594.1 12.4 %convert_bitcast_fusion.6 = (bf16[1,2048,1024]{2,1,0:T(8,128)(2,1)S(1)}, f32[2048,1024]{1,0:T(8,128)S(1)}, bf16[1,2048,1024]{2,1,0:T(8,128)(2,1)}) fusion(f32[]{:T(128)} %bitcast.41, f32[]{:T(128)S(6)} %sub.98, f32[]{:T(128)} %bitcast.42, f32[2048,1024]{1,0:T(8,128)} %get-tuple-element.271, f32[]{:T(128)S(6)} %sub.99, f32[]{:T(128)} %bitcast.43, ...), kind=kLoop, calls=%fused_computation.16.clone.1 | loop fusion | flops 37748736 | bytes 41943076 | tf_op jit(solution)/shard_map/while/body/eval_jaxpr/stack | solution.py:37
  606.5 14.8 %convert_bitcast_fusion.7 = (bf16[1,2048,1024]{2,1,0:T(8,128)(2,1)}, f32[2048,1024]{1,0:T(8,128)}, bf16[1,2048,1024]{2,1,0:T(8,128)(2,1)}) fusion(f32[]{:T(128)} %bitcast.44, f32[]{:T(128)} %bitcast.42, f32[2048,1024]{1,0:T(8,128)} %get-tuple-element.271, f32[]{:T(128)S(6)} %sub.99, f32[]{:T(128)} %bitcast.43, f32[2048,1024]{1,0:T(8,128)} %get-tuple-element.270, ...), kind=kLoop, calls=%fused_computation.15.clone.1 | loop fusion | flops 37748736 | bytes 50331684 | tf_op jit(solution)/shard_map/while/body/eval_jaxpr/stack | solution.py:37
  637.2 12.4 %convert_bitcast_fusion.6 = (bf16[1,2048,1024]{2,1,0:T(8,128)(2,1)S(1)}, f32[2048,1024]{1,0:T(8,128)S(1)}, bf16[1,2048,1024]{2,1,0:T(8,128)(2,1)}) fusion(f32[]{:T(128)} %bitcast.41, f32[]{:T(128)S(6)} %sub.98, f32[]{:T(128)} %bitcast.42, f32[2048,1024]{1,0:T(8,128)} %get-tuple-element.271, f32[]{:T(128)S(6)} %sub.99, f32[]{:T(128)} %bitcast.43, ...), kind=kLoop, calls=%fused_computation.16.clone.1 | loop fusion | flops 37748736 | bytes 41943076 | tf_op jit(solution)/shard_map/while/body/eval_jaxpr/stack | solution.py:37
  649.6 14.8 %convert_bitcast_fusion.7 = (bf16[1,2048,1024]{2,1,0:T(8,128)(2,1)}, f32[2048,1024]{1,0:T(8,128)}, bf16[1,2048,1024]{2,1,0:T(8,128)(2,1)}) fusion(f32[]{:T(128)} %bitcast.44, f32[]{:T(128)} %bitcast.42, f32[2048,1024]{1,0:T(8,128)} %get-tuple-element.271, f32[]{:T(128)S(6)} %sub.99, f32[]{:T(128)} %bitcast.43, f32[2048,1024]{1,0:T(8,128)} %get-tuple-element.270, ...), kind=kLoop, calls=%fused_computation.15.clone.1 | loop fusion | flops 37748736 | bytes 50331684 | tf_op jit(solution)/shard_map/while/body/eval_jaxpr/stack | solution.py:37
  680.3 12.4 %convert_bitcast_fusion.6 = (bf16[1,2048,1024]{2,1,0:T(8,128)(2,1)S(1)}, f32[2048,1024]{1,0:T(8,128)S(1)}, bf16[1,2048,1024]{2,1,0:T(8,128)(2,1)}) fusion(f32[]{:T(128)} %bitcast.41, f32[]{:T(128)S(6)} %sub.98, f32[]{:T(128)} %bitcast.42, f32[2048,1024]{1,0:T(8,128)} %get-tuple-element.271, f32[]{:T(128)S(6)} %sub.99, f32[]{:T(128)} %bitcast.43, ...), kind=kLoop, calls=%fused_computation.16.clone.1 | loop fusion | flops 37748736 | bytes 41943076 | tf_op jit(solution)/shard_map/while/body/eval_jaxpr/stack | solution.py:37
  692.7 14.8 %convert_bitcast_fusion.7 = (bf16[1,2048,1024]{2,1,0:T(8,128)(2,1)}, f32[2048,1024]{1,0:T(8,128)}, bf16[1,2048,1024]{2,1,0:T(8,128)(2,1)}) fusion(f32[]{:T(128)} %bitcast.44, f32[]{:T(128)} %bitcast.42, f32[2048,1024]{1,0:T(8,128)} %get-tuple-element.271, f32[]{:T(128)S(6)} %sub.99, f32[]{:T(128)} %bitcast.43, f32[2048,1024]{1,0:T(8,128)} %get-tuple-element.270, ...), kind=kLoop, calls=%fused_computation.15.clone.1 | loop fusion | flops 37748736 | bytes 50331684 | tf_op jit(solution)/shard_map/while/body/eval_jaxpr/stack | solution.py:37
  723.4 12.4 %convert_bitcast_fusion.6 = (bf16[1,2048,1024]{2,1,0:T(8,128)(2,1)S(1)}, f32[2048,1024]{1,0:T(8,128)S(1)}, bf16[1,2048,1024]{2,1,0:T(8,128)(2,1)}) fusion(f32[]{:T(128)} %bitcast.41, f32[]{:T(128)S(6)} %sub.98, f32[]{:T(128)} %bitcast.42, f32[2048,1024]{1,0:T(8,128)} %get-tuple-element.271, f32[]{:T(128)S(6)} %sub.99, f32[]{:T(128)} %bitcast.43, ...), kind=kLoop, calls=%fused_computation.16.clone.1 | loop fusion | flops 37748736 | bytes 41943076 | tf_op jit(solution)/shard_map/while/body/eval_jaxpr/stack | solution.py:37
  735.8 14.8 %convert_bitcast_fusion.7 = (bf16[1,2048,1024]{2,1,0:T(8,128)(2,1)}, f32[2048,1024]{1,0:T(8,128)}, bf16[1,2048,1024]{2,1,0:T(8,128)(2,1)}) fusion(f32[]{:T(128)} %bitcast.44, f32[]{:T(128)} %bitcast.42, f32[2048,1024]{1,0:T(8,128)} %get-tuple-element.271, f32[]{:T(128)S(6)} %sub.99, f32[]{:T(128)} %bitcast.43, f32[2048,1024]{1,0:T(8,128)} %get-tuple-element.270, ...), kind=kLoop, calls=%fused_computation.15.clone.1 | loop fusion | flops 37748736 | bytes 50331684 | tf_op jit(solution)/shard_map/while/body/eval_jaxpr/stack | solution.py:37
  766.5 12.4 %convert_bitcast_fusion.6 = (bf16[1,2048,1024]{2,1,0:T(8,128)(2,1)S(1)}, f32[2048,1024]{1,0:T(8,128)S(1)}, bf16[1,2048,1024]{2,1,0:T(8,128)(2,1)}) fusion(f32[]{:T(128)} %bitcast.41, f32[]{:T(128)S(6)} %sub.98, f32[]{:T(128)} %bitcast.42, f32[2048,1024]{1,0:T(8,128)} %get-tuple-element.271, f32[]{:T(128)S(6)} %sub.99, f32[]{:T(128)} %bitcast.43, ...), kind=kLoop, calls=%fused_computation.16.clone.1 | loop fusion | flops 37748736 | bytes 41943076 | tf_op jit(solution)/shard_map/while/body/eval_jaxpr/stack | solution.py:37
  779.0 14.8 %convert_bitcast_fusion.7 = (bf16[1,2048,1024]{2,1,0:T(8,128)(2,1)}, f32[2048,1024]{1,0:T(8,128)}, bf16[1,2048,1024]{2,1,0:T(8,128)(2,1)}) fusion(f32[]{:T(128)} %bitcast.44, f32[]{:T(128)} %bitcast.42, f32[2048,1024]{1,0:T(8,128)} %get-tuple-element.271, f32[]{:T(128)S(6)} %sub.99, f32[]{:T(128)} %bitcast.43, f32[2048,1024]{1,0:T(8,128)} %get-tuple-element.270, ...), kind=kLoop, calls=%fused_computation.15.clone.1 | loop fusion | flops 37748736 | bytes 50331684 | tf_op jit(solution)/shard_map/while/body/eval_jaxpr/stack | solution.py:37
  808.4 40.1 %psum.15 = f32[64,192]{1,0:T(8,128)} all-reduce(f32[64,192]{1,0:T(8,128)S(1)} %reshape.51), channel_id=1, replica_groups=mesh['prow'=4,'pcol'=8] {'prow','pcol'}, use_global_device_ids=true, to_apply=%region_4.5 | all-reduce | flops 12288 | bytes 98304 | tf_op jit(solution)/shard_map/psum | solution.py:47
  (176 shorter events, 164.4 us)
Async XLA Ops:
  7.2 115.2 %all-gather.2.cloned.1.call-start = ((), (), s32[]{:S(2)}) async-start(), calls=%async_computation | async-start | bytes 3932160 | tf_op jit(solution)/shard_map/all_gather | solution.py:21
  124.8 10.9 %copy-start.1 = (f32[2048,1024]{1,0:T(8,128)S(1)}, f32[2048,1024]{1,0:T(8,128)}, u32[]{:S(2)}) copy-start(f32[2048,1024]{1,0:T(8,128)} %get-tuple-element.292) | copy-start | bytes 25165828 | tf_op jit(solution)/shard_map/while
  147.0 5.2 copy-start.2
  147.0 6.5 copy-start.3
  162.9 12.4 %copy-start.1 = (f32[2048,1024]{1,0:T(8,128)S(1)}, f32[2048,1024]{1,0:T(8,128)}, u32[]{:S(2)}) copy-start(f32[2048,1024]{1,0:T(8,128)} %get-tuple-element.292) | copy-start | bytes 25165828 | tf_op jit(solution)/shard_map/while
  190.1 5.2 copy-start.2
  190.1 6.5 copy-start.3
  206.0 12.4 %copy-start.1 = (f32[2048,1024]{1,0:T(8,128)S(1)}, f32[2048,1024]{1,0:T(8,128)}, u32[]{:S(2)}) copy-start(f32[2048,1024]{1,0:T(8,128)} %get-tuple-element.292) | copy-start | bytes 25165828 | tf_op jit(solution)/shard_map/while
  233.2 5.2 copy-start.2
  233.2 6.5 copy-start.3
  249.1 12.4 %copy-start.1 = (f32[2048,1024]{1,0:T(8,128)S(1)}, f32[2048,1024]{1,0:T(8,128)}, u32[]{:S(2)}) copy-start(f32[2048,1024]{1,0:T(8,128)} %get-tuple-element.292) | copy-start | bytes 25165828 | tf_op jit(solution)/shard_map/while
  276.4 5.2 copy-start.2
  276.4 6.5 copy-start.3
  292.2 12.4 %copy-start.1 = (f32[2048,1024]{1,0:T(8,128)S(1)}, f32[2048,1024]{1,0:T(8,128)}, u32[]{:S(2)}) copy-start(f32[2048,1024]{1,0:T(8,128)} %get-tuple-element.292) | copy-start | bytes 25165828 | tf_op jit(solution)/shard_map/while
  319.5 5.2 copy-start.2
  319.5 6.5 copy-start.3
  335.3 12.4 %copy-start.1 = (f32[2048,1024]{1,0:T(8,128)S(1)}, f32[2048,1024]{1,0:T(8,128)}, u32[]{:S(2)}) copy-start(f32[2048,1024]{1,0:T(8,128)} %get-tuple-element.292) | copy-start | bytes 25165828 | tf_op jit(solution)/shard_map/while
  362.6 5.2 copy-start.2
  362.6 6.5 copy-start.3
  378.5 12.4 %copy-start.1 = (f32[2048,1024]{1,0:T(8,128)S(1)}, f32[2048,1024]{1,0:T(8,128)}, u32[]{:S(2)}) copy-start(f32[2048,1024]{1,0:T(8,128)} %get-tuple-element.292) | copy-start | bytes 25165828 | tf_op jit(solution)/shard_map/while
  405.7 5.2 copy-start.2
  405.7 6.5 copy-start.3
  421.6 12.4 %copy-start.1 = (f32[2048,1024]{1,0:T(8,128)S(1)}, f32[2048,1024]{1,0:T(8,128)}, u32[]{:S(2)}) copy-start(f32[2048,1024]{1,0:T(8,128)} %get-tuple-element.292) | copy-start | bytes 25165828 | tf_op jit(solution)/shard_map/while
  448.8 5.2 copy-start.2
  448.8 6.5 copy-start.3
  464.7 12.4 %copy-start.1 = (f32[2048,1024]{1,0:T(8,128)S(1)}, f32[2048,1024]{1,0:T(8,128)}, u32[]{:S(2)}) copy-start(f32[2048,1024]{1,0:T(8,128)} %get-tuple-element.292) | copy-start | bytes 25165828 | tf_op jit(solution)/shard_map/while
  492.0 5.2 copy-start.2
  492.0 6.5 copy-start.3
  507.8 12.4 %copy-start.1 = (f32[2048,1024]{1,0:T(8,128)S(1)}, f32[2048,1024]{1,0:T(8,128)}, u32[]{:S(2)}) copy-start(f32[2048,1024]{1,0:T(8,128)} %get-tuple-element.292) | copy-start | bytes 25165828 | tf_op jit(solution)/shard_map/while
  535.1 5.2 copy-start.2
  535.1 6.5 copy-start.3
  550.9 12.4 %copy-start.1 = (f32[2048,1024]{1,0:T(8,128)S(1)}, f32[2048,1024]{1,0:T(8,128)}, u32[]{:S(2)}) copy-start(f32[2048,1024]{1,0:T(8,128)} %get-tuple-element.292) | copy-start | bytes 25165828 | tf_op jit(solution)/shard_map/while
  578.2 5.2 copy-start.2
  578.2 6.5 copy-start.3
  594.1 12.4 %copy-start.1 = (f32[2048,1024]{1,0:T(8,128)S(1)}, f32[2048,1024]{1,0:T(8,128)}, u32[]{:S(2)}) copy-start(f32[2048,1024]{1,0:T(8,128)} %get-tuple-element.292) | copy-start | bytes 25165828 | tf_op jit(solution)/shard_map/while
  621.3 5.2 copy-start.2
  621.3 6.5 copy-start.3
  637.2 12.4 %copy-start.1 = (f32[2048,1024]{1,0:T(8,128)S(1)}, f32[2048,1024]{1,0:T(8,128)}, u32[]{:S(2)}) copy-start(f32[2048,1024]{1,0:T(8,128)} %get-tuple-element.292) | copy-start | bytes 25165828 | tf_op jit(solution)/shard_map/while
  664.4 5.2 copy-start.2
  664.4 6.5 copy-start.3
  680.3 12.4 %copy-start.1 = (f32[2048,1024]{1,0:T(8,128)S(1)}, f32[2048,1024]{1,0:T(8,128)}, u32[]{:S(2)}) copy-start(f32[2048,1024]{1,0:T(8,128)} %get-tuple-element.292) | copy-start | bytes 25165828 | tf_op jit(solution)/shard_map/while
  707.6 5.2 copy-start.2
  707.6 6.5 copy-start.3
  723.4 12.4 %copy-start.1 = (f32[2048,1024]{1,0:T(8,128)S(1)}, f32[2048,1024]{1,0:T(8,128)}, u32[]{:S(2)}) copy-start(f32[2048,1024]{1,0:T(8,128)} %get-tuple-element.292) | copy-start | bytes 25165828 | tf_op jit(solution)/shard_map/while
  750.7 5.2 copy-start.2
  750.7 6.5 copy-start.3
  766.5 12.4 %copy-start.1 = (f32[2048,1024]{1,0:T(8,128)S(1)}, f32[2048,1024]{1,0:T(8,128)}, u32[]{:S(2)}) copy-start(f32[2048,1024]{1,0:T(8,128)} %get-tuple-element.292) | copy-start | bytes 25165828 | tf_op jit(solution)/shard_map/while
  793.8 6.5 copy-start.3
  (2 other events, 6.2 us)
Sparse Core Ops, SparseCore 0:
  94.8 27.5 all-gather.1
where the time goes:
time: 856 us; the launch traced here: 855 us
  other arithmetic  436 us (51%)
  matrix products  131 us (15%)
  local copies, waits for them, and re-layouts  124 us (14%)
  blocking collectives  123 us (14%)
  waiting for transfers between devices  16.7 us (2%)
  between operations  14.1 us (2%)
  loops' own time  10.5 us (1%)
    another operation x32, other arithmetic, advance(): stacked = jnp.stack(term_list)  431 us
    dot_general x16, matrix products, advance(): jnp.einsum('grc,cm->grm', stacked, filtered_cols, preferred_element_type=...  127 us
    while x112, local copies, waits for them, and re-layouts  104 us
    psum x1, blocking collectives, per_device(): filtered = lax.psum(partial_value, 'pcol').astype(jnp.bfloat16)  82.8 us
    psum x1, blocking collectives, per_device(): spectra = lax.psum(partial_spectra.reshape(L, -1), ('prow', 'pcol'))  40.1 us
  transfers between devices with their start and end apart: 1, of which 1 were waited for; matrix products, arithmetic and copies ran while one was open for 1% of the time, Pallas kernels for 0%

commit v1 on v0

--- a/solution.py
+++ b/solution.py
@@ -16,7 +16,7 @@
 def per_device(inverse_cov, cosines, sky_maps):
     cols_here = inverse_cov.shape[1]
     partial_value = jnp.dot(inverse_cov, sky_maps, preferred_element_type=jnp.float32)
-    filtered = lax.psum(partial_value, "pcol").astype(jnp.bfloat16)
+    filtered = jnp.sum(lax.all_gather(partial_value, "pcol"), axis=0).astype(jnp.bfloat16)
     column_index = lax.axis_index("pcol")
     full_maps = lax.all_gather(filtered, "prow", axis=0, tiled=True)
     filtered_cols = lax.dynamic_slice_in_dim(full_maps, column_index * cols_here, cols_here, 0)

time: 856 us -> 981 us (1.15)
  waiting for transfers between devices: 16.7 us -> 196 us
  blocking collectives: 123 us -> 40.1 us
  local copies, waits for them, and re-layouts: 124 us -> 145 us
    all_gather x0 -> x1, waiting for transfers between devices: none -> 179 us  [per_device(): lax.all_gather(partial_value, 'pcol')]
    psum x1 -> x0, blocking collectives: 82.8 us -> none  [per_device(): filtered = lax.psum(partial_value, 'pcol').astype(jnp.bfloat16)]
    unnamed x3 -> x8, local copies, waits for them, and re-layouts: 9.44 us -> 30.5 us
  transfers between devices with their start and end apart: 1 -> 2, of which waited for: 1 -> 2; matrix products, arithmetic and copies ran while one was open for 1% -> 1% of each run, Pallas kernels for 0% -> 0%
where the time goes in v1:
time: 981 us; the launch traced here: 980 us
  other arithmetic  444 us (45%)
  waiting for transfers between devices  196 us (20%)
  local copies, waits for them, and re-layouts  145 us (15%)
  matrix products  132 us (13%)
  blocking collectives  40.1 us (4%)
  between operations  14.1 us (1%)
    another operation x32, other arithmetic, advance(): stacked = jnp.stack(term_list)  431 us
    all_gather x1, waiting for transfers between devices, per_device(): lax.all_gather(partial_value, 'pcol')  179 us
    dot_general x16, matrix products, advance(): jnp.einsum('grc,cm->grm', stacked, filtered_cols, preferred_element_type=...  127 us
    while x112, local copies, waits for them, and re-layouts  104 us
    psum x1, blocking collectives, per_device(): spectra = lax.psum(partial_spectra.reshape(L, -1), ('prow', 'pcol'))  40.1 us
    unnamed x8, local copies, waits for them, and re-layouts  30.5 us
  transfers between devices with their start and end apart: 2, of which 2 were waited for; matrix products, arithmetic and copies ran while one was open for 1% of the time, Pallas kernels for 0%

profile of v1, /device:TPU:0, one launch (start us, length us, event | category | flops | bytes accessed | tf_op | source)
XLA Modules:
  0.0 980.5 jit_solution(6749792837446851162)
XLA Ops:
  13.1 178.9 %all-gather.6.cloned.1.call-done = f32[16384,192]{0,1:T(8,128)} async-done(((f32[2048,192]{0,1:T(8,128)}), f32[16384,192]{0,1:T(8,128)}) %all-gather.6.cloned.1.call-update) | async-done | bytes 12582928 | tf_op jit(solution)/shard_map/all_gather | solution.py:19
  192.1 21.0 %copy.5 = f32[24,8,8,2048]{3,2,1,0:T(8,128)} copy(f32[24,8,8,2048]{3,1,2,0:T(8,128)} %bitcast.54) | data formatting | bytes 25165824
  213.1 8.7 bitcast_reduce_fusion
  221.8 8.5 copy.9
  231.7 16.9 %all-gather.4.cloned.1.call-done = bf16[8192,192]{0,1:T(8,128)(2,1)} async-done(((bf16[2048,192]{0,1:T(8,128)(2,1)}), bf16[8192,192]{0,1:T(8,128)(2,1)}) %all-gather.4.cloned.1.call-update) | async-done | bytes 3145744 | tf_op jit(solution)/shard_map/all_gather | solution.py:21
  249.7 683.9 %while.18 = (s32[]{:T(128)}, f32[2048,1024]{1,0:T(8,128)}, f32[2048,1024]{1,0:T(8,128)}, f32[16,4,192]{2,1,0:T(4,128)S(1)}, s32[16]{0:T(128)S(1)}, /*index=5*/f3...) while((s32[]{:T(128)}, f32[2048,1024]{1,0:T(8,128)}, ...), condition=%wide.region_3.4_spmd.clone, body=%wide.region_1.3_spmd.clone.sunk | while | flops 3325034496 | bytes 194916608 | solution.py:44
  250.9 10.9 %convert_bitcast_fusion.6 = (bf16[1,2048,1024]{2,1,0:T(8,128)(2,1)S(1)}, f32[2048,1024]{1,0:T(8,128)S(1)}, bf16[1,2048,1024]{2,1,0:T(8,128)(2,1)}) fusion(f32[]{:T(128)} %bitcast.46, f32[]{:T(128)S(6)} %sub.98, f32[]{:T(128)} %bitcast.47, f32[2048,1024]{1,0:T(8,128)} %get-tuple-element.271, f32[]{:T(128)S(6)} %sub.99, f32[]{:T(128)} %bitcast.48, ...), kind=kLoop, calls=%fused_computation.16.clone.1 | loop fusion | flops 37748736 | bytes 41943076 | tf_op jit(solution)/shard_map/while/body/eval_jaxpr/stack | solution.py:37
  261.8 11.3 %convert_bitcast_fusion.7 = (bf16[1,2048,1024]{2,1,0:T(8,128)(2,1)}, f32[2048,1024]{1,0:T(8,128)}, bf16[1,2048,1024]{2,1,0:T(8,128)(2,1)}) fusion(f32[]{:T(128)} %bitcast.49, f32[]{:T(128)} %bitcast.47, f32[2048,1024]{1,0:T(8,128)} %get-tuple-element.271, f32[]{:T(128)S(6)} %sub.99, f32[]{:T(128)} %bitcast.48, f32[2048,1024]{1,0:T(8,128)} %get-tuple-element.270, ...), kind=kLoop, calls=%fused_computation.15.clone.1 | loop fusion | flops 37748736 | bytes 50331684 | tf_op jit(solution)/shard_map/while/body/eval_jaxpr/stack | solution.py:37
  288.9 12.4 %convert_bitcast_fusion.6 = (bf16[1,2048,1024]{2,1,0:T(8,128)(2,1)S(1)}, f32[2048,1024]{1,0:T(8,128)S(1)}, bf16[1,2048,1024]{2,1,0:T(8,128)(2,1)}) fusion(f32[]{:T(128)} %bitcast.46, f32[]{:T(128)S(6)} %sub.98, f32[]{:T(128)} %bitcast.47, f32[2048,1024]{1,0:T(8,128)} %get-tuple-element.271, f32[]{:T(128)S(6)} %sub.99, f32[]{:T(128)} %bitcast.48, ...), kind=kLoop, calls=%fused_computation.16.clone.1 | loop fusion | flops 37748736 | bytes 41943076 | tf_op jit(solution)/shard_map/while/body/eval_jaxpr/stack | solution.py:37
  301.4 14.8 %convert_bitcast_fusion.7 = (bf16[1,2048,1024]{2,1,0:T(8,128)(2,1)}, f32[2048,1024]{1,0:T(8,128)}, bf16[1,2048,1024]{2,1,0:T(8,128)(2,1)}) fusion(f32[]{:T(128)} %bitcast.49, f32[]{:T(128)} %bitcast.47, f32[2048,1024]{1,0:T(8,128)} %get-tuple-element.271, f32[]{:T(128)S(6)} %sub.99, f32[]{:T(128)} %bitcast.48, f32[2048,1024]{1,0:T(8,128)} %get-tuple-element.270, ...), kind=kLoop, calls=%fused_computation.15.clone.1 | loop fusion | flops 37748736 | bytes 50331684 | tf_op jit(solution)/shard_map/while/body/eval_jaxpr/stack | solution.py:37
  322.7 8.0 multiply_reduce_fusion.2
  332.0 12.4 %convert_bitcast_fusion.6 = (bf16[1,2048,1024]{2,1,0:T(8,128)(2,1)S(1)}, f32[2048,1024]{1,0:T(8,128)S(1)}, bf16[1,2048,1024]{2,1,0:T(8,128)(2,1)}) fusion(f32[]{:T(128)} %bitcast.46, f32[]{:T(128)S(6)} %sub.98, f32[]{:T(128)} %bitcast.47, f32[2048,1024]{1,0:T(8,128)} %get-tuple-element.271, f32[]{:T(128)S(6)} %sub.99, f32[]{:T(128)} %bitcast.48, ...), kind=kLoop, calls=%fused_computation.16.clone.1 | loop fusion | flops 37748736 | bytes 41943076 | tf_op jit(solution)/shard_map/while/body/eval_jaxpr/stack | solution.py:37
  344.4 14.8 %convert_bitcast_fusion.7 = (bf16[1,2048,1024]{2,1,0:T(8,128)(2,1)}, f32[2048,1024]{1,0:T(8,128)}, bf16[1,2048,1024]{2,1,0:T(8,128)(2,1)}) fusion(f32[]{:T(128)} %bitcast.49, f32[]{:T(128)} %bitcast.47, f32[2048,1024]{1,0:T(8,128)} %get-tuple-element.271, f32[]{:T(128)S(6)} %sub.99, f32[]{:T(128)} %bitcast.48, f32[2048,1024]{1,0:T(8,128)} %get-tuple-element.270, ...), kind=kLoop, calls=%fused_computation.15.clone.1 | loop fusion | flops 37748736 | bytes 50331684 | tf_op jit(solution)/shard_map/while/body/eval_jaxpr/stack | solution.py:37
  365.7 8.0 multiply_reduce_fusion.2
  375.0 12.4 %convert_bitcast_fusion.6 = (bf16[1,2048,1024]{2,1,0:T(8,128)(2,1)S(1)}, f32[2048,1024]{1,0:T(8,128)S(1)}, bf16[1,2048,1024]{2,1,0:T(8,128)(2,1)}) fusion(f32[]{:T(128)} %bitcast.46, f32[]{:T(128)S(6)} %sub.98, f32[]{:T(128)} %bitcast.47, f32[2048,1024]{1,0:T(8,128)} %get-tuple-element.271, f32[]{:T(128)S(6)} %sub.99, f32[]{:T(128)} %bitcast.48, ...), kind=kLoop, calls=%fused_computation.16.clone.1 | loop fusion | flops 37748736 | bytes 41943076 | tf_op jit(solution)/shard_map/while/body/eval_jaxpr/stack | solution.py:37
  387.5 14.8 %convert_bitcast_fusion.7 = (bf16[1,2048,1024]{2,1,0:T(8,128)(2,1)}, f32[2048,1024]{1,0:T(8,128)}, bf16[1,2048,1024]{2,1,0:T(8,128)(2,1)}) fusion(f32[]{:T(128)} %bitcast.49, f32[]{:T(128)} %bitcast.47, f32[2048,1024]{1,0:T(8,128)} %get-tuple-element.271, f32[]{:T(128)S(6)} %sub.99, f32[]{:T(128)} %bitcast.48, f32[2048,1024]{1,0:T(8,128)} %get-tuple-element.270, ...), kind=kLoop, calls=%fused_computation.15.clone.1 | loop fusion | flops 37748736 | bytes 50331684 | tf_op jit(solution)/shard_map/while/body/eval_jaxpr/stack | solution.py:37
  408.8 8.0 multiply_reduce_fusion.2
  418.1 12.4 %convert_bitcast_fusion.6 = (bf16[1,2048,1024]{2,1,0:T(8,128)(2,1)S(1)}, f32[2048,1024]{1,0:T(8,128)S(1)}, bf16[1,2048,1024]{2,1,0:T(8,128)(2,1)}) fusion(f32[]{:T(128)} %bitcast.46, f32[]{:T(128)S(6)} %sub.98, f32[]{:T(128)} %bitcast.47, f32[2048,1024]{1,0:T(8,128)} %get-tuple-element.271, f32[]{:T(128)S(6)} %sub.99, f32[]{:T(128)} %bitcast.48, ...), kind=kLoop, calls=%fused_computation.16.clone.1 | loop fusion | flops 37748736 | bytes 41943076 | tf_op jit(solution)/shard_map/while/body/eval_jaxpr/stack | solution.py:37
  430.5 14.8 %convert_bitcast_fusion.7 = (bf16[1,2048,1024]{2,1,0:T(8,128)(2,1)}, f32[2048,1024]{1,0:T(8,128)}, bf16[1,2048,1024]{2,1,0:T(8,128)(2,1)}) fusion(f32[]{:T(128)} %bitcast.49, f32[]{:T(128)} %bitcast.47, f32[2048,1024]{1,0:T(8,128)} %get-tuple-element.271, f32[]{:T(128)S(6)} %sub.99, f32[]{:T(128)} %bitcast.48, f32[2048,1024]{1,0:T(8,128)} %get-tuple-element.270, ...), kind=kLoop, calls=%fused_computation.15.clone.1 | loop fusion | flops 37748736 | bytes 50331684 | tf_op jit(solution)/shard_map/while/body/eval_jaxpr/stack | solution.py:37
  451.9 8.0 multiply_reduce_fusion.2
  461.1 12.4 %convert_bitcast_fusion.6 = (bf16[1,2048,1024]{2,1,0:T(8,128)(2,1)S(1)}, f32[2048,1024]{1,0:T(8,128)S(1)}, bf16[1,2048,1024]{2,1,0:T(8,128)(2,1)}) fusion(f32[]{:T(128)} %bitcast.46, f32[]{:T(128)S(6)} %sub.98, f32[]{:T(128)} %bitcast.47, f32[2048,1024]{1,0:T(8,128)} %get-tuple-element.271, f32[]{:T(128)S(6)} %sub.99, f32[]{:T(128)} %bitcast.48, ...), kind=kLoop, calls=%fused_computation.16.clone.1 | loop fusion | flops 37748736 | bytes 41943076 | tf_op jit(solution)/shard_map/while/body/eval_jaxpr/stack | solution.py:37
  473.6 14.8 %convert_bitcast_fusion.7 = (bf16[1,2048,1024]{2,1,0:T(8,128)(2,1)}, f32[2048,1024]{1,0:T(8,128)}, bf16[1,2048,1024]{2,1,0:T(8,128)(2,1)}) fusion(f32[]{:T(128)} %bitcast.49, f32[]{:T(128)} %bitcast.47, f32[2048,1024]{1,0:T(8,128)} %get-tuple-element.271, f32[]{:T(128)S(6)} %sub.99, f32[]{:T(128)} %bitcast.48, f32[2048,1024]{1,0:T(8,128)} %get-tuple-element.270, ...), kind=kLoop, calls=%fused_computation.15.clone.1 | loop fusion | flops 37748736 | bytes 50331684 | tf_op jit(solution)/shard_map/while/body/eval_jaxpr/stack | solution.py:37
  494.9 8.0 multiply_reduce_fusion.2
  504.2 12.4 %convert_bitcast_fusion.6 = (bf16[1,2048,1024]{2,1,0:T(8,128)(2,1)S(1)}, f32[2048,1024]{1,0:T(8,128)S(1)}, bf16[1,2048,1024]{2,1,0:T(8,128)(2,1)}) fusion(f32[]{:T(128)} %bitcast.46, f32[]{:T(128)S(6)} %sub.98, f32[]{:T(128)} %bitcast.47, f32[2048,1024]{1,0:T(8,128)} %get-tuple-element.271, f32[]{:T(128)S(6)} %sub.99, f32[]{:T(128)} %bitcast.48, ...), kind=kLoop, calls=%fused_computation.16.clone.1 | loop fusion | flops 37748736 | bytes 41943076 | tf_op jit(solution)/shard_map/while/body/eval_jaxpr/stack | solution.py:37
  516.6 14.8 %convert_bitcast_fusion.7 = (bf16[1,2048,1024]{2,1,0:T(8,128)(2,1)}, f32[2048,1024]{1,0:T(8,128)}, bf16[1,2048,1024]{2,1,0:T(8,128)(2,1)}) fusion(f32[]{:T(128)} %bitcast.49, f32[]{:T(128)} %bitcast.47, f32[2048,1024]{1,0:T(8,128)} %get-tuple-element.271, f32[]{:T(128)S(6)} %sub.99, f32[]{:T(128)} %bitcast.48, f32[2048,1024]{1,0:T(8,128)} %get-tuple-element.270, ...), kind=kLoop, calls=%fused_computation.15.clone.1 | loop fusion | flops 37748736 | bytes 50331684 | tf_op jit(solution)/shard_map/while/body/eval_jaxpr/stack | solution.py:37
  538.0 8.0 multiply_reduce_fusion.2
  547.3 12.4 %convert_bitcast_fusion.6 = (bf16[1,2048,1024]{2,1,0:T(8,128)(2,1)S(1)}, f32[2048,1024]{1,0:T(8,128)S(1)}, bf16[1,2048,1024]{2,1,0:T(8,128)(2,1)}) fusion(f32[]{:T(128)} %bitcast.46, f32[]{:T(128)S(6)} %sub.98, f32[]{:T(128)} %bitcast.47, f32[2048,1024]{1,0:T(8,128)} %get-tuple-element.271, f32[]{:T(128)S(6)} %sub.99, f32[]{:T(128)} %bitcast.48, ...), kind=kLoop, calls=%fused_computation.16.clone.1 | loop fusion | flops 37748736 | bytes 41943076 | tf_op jit(solution)/shard_map/while/body/eval_jaxpr/stack | solution.py:37
  559.7 14.8 %convert_bitcast_fusion.7 = (bf16[1,2048,1024]{2,1,0:T(8,128)(2,1)}, f32[2048,1024]{1,0:T(8,128)}, bf16[1,2048,1024]{2,1,0:T(8,128)(2,1)}) fusion(f32[]{:T(128)} %bitcast.49, f32[]{:T(128)} %bitcast.47, f32[2048,1024]{1,0:T(8,128)} %get-tuple-element.271, f32[]{:T(128)S(6)} %sub.99, f32[]{:T(128)} %bitcast.48, f32[2048,1024]{1,0:T(8,128)} %get-tuple-element.270, ...), kind=kLoop, calls=%fused_computation.15.clone.1 | loop fusion | flops 37748736 | bytes 50331684 | tf_op jit(solution)/shard_map/while/body/eval_jaxpr/stack | solution.py:37
  581.0 8.0 multiply_reduce_fusion.2
  590.3 12.4 %convert_bitcast_fusion.6 = (bf16[1,2048,1024]{2,1,0:T(8,128)(2,1)S(1)}, f32[2048,1024]{1,0:T(8,128)S(1)}, bf16[1,2048,1024]{2,1,0:T(8,128)(2,1)}) fusion(f32[]{:T(128)} %bitcast.46, f32[]{:T(128)S(6)} %sub.98, f32[]{:T(128)} %bitcast.47, f32[2048,1024]{1,0:T(8,128)} %get-tuple-element.271, f32[]{:T(128)S(6)} %sub.99, f32[]{:T(128)} %bitcast.48, ...), kind=kLoop, calls=%fused_computation.16.clone.1 | loop fusion | flops 37748736 | bytes 41943076 | tf_op jit(solution)/shard_map/while/body/eval_jaxpr/stack | solution.py:37
  602.8 14.8 %convert_bitcast_fusion.7 = (bf16[1,2048,1024]{2,1,0:T(8,128)(2,1)}, f32[2048,1024]{1,0:T(8,128)}, bf16[1,2048,1024]{2,1,0:T(8,128)(2,1)}) fusion(f32[]{:T(128)} %bitcast.49, f32[]{:T(128)} %bitcast.47, f32[2048,1024]{1,0:T(8,128)} %get-tuple-element.271, f32[]{:T(128)S(6)} %sub.99, f32[]{:T(128)} %bitcast.48, f32[2048,1024]{1,0:T(8,128)} %get-tuple-element.270, ...), kind=kLoop, calls=%fused_computation.15.clone.1 | loop fusion | flops 37748736 | bytes 50331684 | tf_op jit(solution)/shard_map/while/body/eval_jaxpr/stack | solution.py:37
  624.1 8.0 multiply_reduce_fusion.2
  633.4 12.4 %convert_bitcast_fusion.6 = (bf16[1,2048,1024]{2,1,0:T(8,128)(2,1)S(1)}, f32[2048,1024]{1,0:T(8,128)S(1)}, bf16[1,2048,1024]{2,1,0:T(8,128)(2,1)}) fusion(f32[]{:T(128)} %bitcast.46, f32[]{:T(128)S(6)} %sub.98, f32[]{:T(128)} %bitcast.47, f32[2048,1024]{1,0:T(8,128)} %get-tuple-element.271, f32[]{:T(128)S(6)} %sub.99, f32[]{:T(128)} %bitcast.48, ...), kind=kLoop, calls=%fused_computation.16.clone.1 | loop fusion | flops 37748736 | bytes 41943076 | tf_op jit(solution)/shard_map/while/body/eval_jaxpr/stack | solution.py:37
  645.8 14.8 %convert_bitcast_fusion.7 = (bf16[1,2048,1024]{2,1,0:T(8,128)(2,1)}, f32[2048,1024]{1,0:T(8,128)}, bf16[1,2048,1024]{2,1,0:T(8,128)(2,1)}) fusion(f32[]{:T(128)} %bitcast.49, f32[]{:T(128)} %bitcast.47, f32[2048,1024]{1,0:T(8,128)} %get-tuple-element.271, f32[]{:T(128)S(6)} %sub.99, f32[]{:T(128)} %bitcast.48, f32[2048,1024]{1,0:T(8,128)} %get-tuple-element.270, ...), kind=kLoop, calls=%fused_computation.15.clone.1 | loop fusion | flops 37748736 | bytes 50331684 | tf_op jit(solution)/shard_map/while/body/eval_jaxpr/stack | solution.py:37
  667.1 8.0 multiply_reduce_fusion.2
  676.4 12.4 %convert_bitcast_fusion.6 = (bf16[1,2048,1024]{2,1,0:T(8,128)(2,1)S(1)}, f32[2048,1024]{1,0:T(8,128)S(1)}, bf16[1,2048,1024]{2,1,0:T(8,128)(2,1)}) fusion(f32[]{:T(128)} %bitcast.46, f32[]{:T(128)S(6)} %sub.98, f32[]{:T(128)} %bitcast.47, f32[2048,1024]{1,0:T(8,128)} %get-tuple-element.271, f32[]{:T(128)S(6)} %sub.99, f32[]{:T(128)} %bitcast.48, ...), kind=kLoop, calls=%fused_computation.16.clone.1 | loop fusion | flops 37748736 | bytes 41943076 | tf_op jit(solution)/shard_map/while/body/eval_jaxpr/stack | solution.py:37
  688.9 14.8 %convert_bitcast_fusion.7 = (bf16[1,2048,1024]{2,1,0:T(8,128)(2,1)}, f32[2048,1024]{1,0:T(8,128)}, bf16[1,2048,1024]{2,1,0:T(8,128)(2,1)}) fusion(f32[]{:T(128)} %bitcast.49, f32[]{:T(128)} %bitcast.47, f32[2048,1024]{1,0:T(8,128)} %get-tuple-element.271, f32[]{:T(128)S(6)} %sub.99, f32[]{:T(128)} %bitcast.48, f32[2048,1024]{1,0:T(8,128)} %get-tuple-element.270, ...), kind=kLoop, calls=%fused_computation.15.clone.1 | loop fusion | flops 37748736 | bytes 50331684 | tf_op jit(solution)/shard_map/while/body/eval_jaxpr/stack | solution.py:37
  719.5 12.4 %convert_bitcast_fusion.6 = (bf16[1,2048,1024]{2,1,0:T(8,128)(2,1)S(1)}, f32[2048,1024]{1,0:T(8,128)S(1)}, bf16[1,2048,1024]{2,1,0:T(8,128)(2,1)}) fusion(f32[]{:T(128)} %bitcast.46, f32[]{:T(128)S(6)} %sub.98, f32[]{:T(128)} %bitcast.47, f32[2048,1024]{1,0:T(8,128)} %get-tuple-element.271, f32[]{:T(128)S(6)} %sub.99, f32[]{:T(128)} %bitcast.48, ...), kind=kLoop, calls=%fused_computation.16.clone.1 | loop fusion | flops 37748736 | bytes 41943076 | tf_op jit(solution)/shard_map/while/body/eval_jaxpr/stack | solution.py:37
  731.9 14.8 %convert_bitcast_fusion.7 = (bf16[1,2048,1024]{2,1,0:T(8,128)(2,1)}, f32[2048,1024]{1,0:T(8,128)}, bf16[1,2048,1024]{2,1,0:T(8,128)(2,1)}) fusion(f32[]{:T(128)} %bitcast.49, f32[]{:T(128)} %bitcast.47, f32[2048,1024]{1,0:T(8,128)} %get-tuple-element.271, f32[]{:T(128)S(6)} %sub.99, f32[]{:T(128)} %bitcast.48, f32[2048,1024]{1,0:T(8,128)} %get-tuple-element.270, ...), kind=kLoop, calls=%fused_computation.15.clone.1 | loop fusion | flops 37748736 | bytes 50331684 | tf_op jit(solution)/shard_map/while/body/eval_jaxpr/stack | solution.py:37
  762.5 12.4 %convert_bitcast_fusion.6 = (bf16[1,2048,1024]{2,1,0:T(8,128)(2,1)S(1)}, f32[2048,1024]{1,0:T(8,128)S(1)}, bf16[1,2048,1024]{2,1,0:T(8,128)(2,1)}) fusion(f32[]{:T(128)} %bitcast.46, f32[]{:T(128)S(6)} %sub.98, f32[]{:T(128)} %bitcast.47, f32[2048,1024]{1,0:T(8,128)} %get-tuple-element.271, f32[]{:T(128)S(6)} %sub.99, f32[]{:T(128)} %bitcast.48, ...), kind=kLoop, calls=%fused_computation.16.clone.1 | loop fusion | flops 37748736 | bytes 41943076 | tf_op jit(solution)/shard_map/while/body/eval_jaxpr/stack | solution.py:37
  775.0 14.8 %convert_bitcast_fusion.7 = (bf16[1,2048,1024]{2,1,0:T(8,128)(2,1)}, f32[2048,1024]{1,0:T(8,128)}, bf16[1,2048,1024]{2,1,0:T(8,128)(2,1)}) fusion(f32[]{:T(128)} %bitcast.49, f32[]{:T(128)} %bitcast.47, f32[2048,1024]{1,0:T(8,128)} %get-tuple-element.271, f32[]{:T(128)S(6)} %sub.99, f32[]{:T(128)} %bitcast.48, f32[2048,1024]{1,0:T(8,128)} %get-tuple-element.270, ...), kind=kLoop, calls=%fused_computation.15.clone.1 | loop fusion | flops 37748736 | bytes 50331684 | tf_op jit(solution)/shard_map/while/body/eval_jaxpr/stack | solution.py:37
  805.6 12.4 %convert_bitcast_fusion.6 = (bf16[1,2048,1024]{2,1,0:T(8,128)(2,1)S(1)}, f32[2048,1024]{1,0:T(8,128)S(1)}, bf16[1,2048,1024]{2,1,0:T(8,128)(2,1)}) fusion(f32[]{:T(128)} %bitcast.46, f32[]{:T(128)S(6)} %sub.98, f32[]{:T(128)} %bitcast.47, f32[2048,1024]{1,0:T(8,128)} %get-tuple-element.271, f32[]{:T(128)S(6)} %sub.99, f32[]{:T(128)} %bitcast.48, ...), kind=kLoop, calls=%fused_computation.16.clone.1 | loop fusion | flops 37748736 | bytes 41943076 | tf_op jit(solution)/shard_map/while/body/eval_jaxpr/stack | solution.py:37
  818.0 14.8 %convert_bitcast_fusion.7 = (bf16[1,2048,1024]{2,1,0:T(8,128)(2,1)}, f32[2048,1024]{1,0:T(8,128)}, bf16[1,2048,1024]{2,1,0:T(8,128)(2,1)}) fusion(f32[]{:T(128)} %bitcast.49, f32[]{:T(128)} %bitcast.47, f32[2048,1024]{1,0:T(8,128)} %get-tuple-element.271, f32[]{:T(128)S(6)} %sub.99, f32[]{:T(128)} %bitcast.48, f32[2048,1024]{1,0:T(8,128)} %get-tuple-element.270, ...), kind=kLoop, calls=%fused_computation.15.clone.1 | loop fusion | flops 37748736 | bytes 50331684 | tf_op jit(solution)/shard_map/while/body/eval_jaxpr/stack | solution.py:37
  848.7 12.4 %convert_bitcast_fusion.6 = (bf16[1,2048,1024]{2,1,0:T(8,128)(2,1)S(1)}, f32[2048,1024]{1,0:T(8,128)S(1)}, bf16[1,2048,1024]{2,1,0:T(8,128)(2,1)}) fusion(f32[]{:T(128)} %bitcast.46, f32[]{:T(128)S(6)} %sub.98, f32[]{:T(128)} %bitcast.47, f32[2048,1024]{1,0:T(8,128)} %get-tuple-element.271, f32[]{:T(128)S(6)} %sub.99, f32[]{:T(128)} %bitcast.48, ...), kind=kLoop, calls=%fused_computation.16.clone.1 | loop fusion | flops 37748736 | bytes 41943076 | tf_op jit(solution)/shard_map/while/body/eval_jaxpr/stack | solution.py:37
  861.1 14.8 %convert_bitcast_fusion.7 = (bf16[1,2048,1024]{2,1,0:T(8,128)(2,1)}, f32[2048,1024]{1,0:T(8,128)}, bf16[1,2048,1024]{2,1,0:T(8,128)(2,1)}) fusion(f32[]{:T(128)} %bitcast.49, f32[]{:T(128)} %bitcast.47, f32[2048,1024]{1,0:T(8,128)} %get-tuple-element.271, f32[]{:T(128)S(6)} %sub.99, f32[]{:T(128)} %bitcast.48, f32[2048,1024]{1,0:T(8,128)} %get-tuple-element.270, ...), kind=kLoop, calls=%fused_computation.15.clone.1 | loop fusion | flops 37748736 | bytes 50331684 | tf_op jit(solution)/shard_map/while/body/eval_jaxpr/stack | solution.py:37
  891.7 12.4 %convert_bitcast_fusion.6 = (bf16[1,2048,1024]{2,1,0:T(8,128)(2,1)S(1)}, f32[2048,1024]{1,0:T(8,128)S(1)}, bf16[1,2048,1024]{2,1,0:T(8,128)(2,1)}) fusion(f32[]{:T(128)} %bitcast.46, f32[]{:T(128)S(6)} %sub.98, f32[]{:T(128)} %bitcast.47, f32[2048,1024]{1,0:T(8,128)} %get-tuple-element.271, f32[]{:T(128)S(6)} %sub.99, f32[]{:T(128)} %bitcast.48, ...), kind=kLoop, calls=%fused_computation.16.clone.1 | loop fusion | flops 37748736 | bytes 41943076 | tf_op jit(solution)/shard_map/while/body/eval_jaxpr/stack | solution.py:37
  904.1 14.8 %convert_bitcast_fusion.7 = (bf16[1,2048,1024]{2,1,0:T(8,128)(2,1)}, f32[2048,1024]{1,0:T(8,128)}, bf16[1,2048,1024]{2,1,0:T(8,128)(2,1)}) fusion(f32[]{:T(128)} %bitcast.49, f32[]{:T(128)} %bitcast.47, f32[2048,1024]{1,0:T(8,128)} %get-tuple-element.271, f32[]{:T(128)S(6)} %sub.99, f32[]{:T(128)} %bitcast.48, f32[2048,1024]{1,0:T(8,128)} %get-tuple-element.270, ...), kind=kLoop, calls=%fused_computation.15.clone.1 | loop fusion | flops 37748736 | bytes 50331684 | tf_op jit(solution)/shard_map/while/body/eval_jaxpr/stack | solution.py:37
  933.6 40.1 %psum.7 = f32[64,192]{1,0:T(8,128)} all-reduce(f32[64,192]{1,0:T(8,128)S(1)} %reshape.51), channel_id=1, replica_groups=mesh['prow'=4,'pcol'=8] {'prow','pcol'}, use_global_device_ids=true, to_apply=%region_4.5 | all-reduce | flops 12288 | bytes 98304 | tf_op jit(solution)/shard_map/psum | solution.py:47
  (184 shorter events, 179.8 us)
Async XLA Ops:
  7.2 184.9 %all-gather.6.cloned.1.call-start = ((), (), s32[]{:S(2)}) async-start(), calls=%async_computation.1 | async-start | bytes 14155776 | tf_op jit(solution)/shard_map/all_gather | solution.py:19
  13.1 235.5 %all-gather.4.cloned.1.call-start = ((), (), s32[]{:S(2)}) async-start(), calls=%async_computation | async-start | bytes 3932160 | tf_op jit(solution)/shard_map/all_gather | solution.py:21
  221.8 8.5 copy-start.5
  250.9 10.9 %copy-start.2 = (f32[2048,1024]{1,0:T(8,128)S(1)}, f32[2048,1024]{1,0:T(8,128)}, u32[]{:S(2)}) copy-start(f32[2048,1024]{1,0:T(8,128)} %get-tuple-element.292) | copy-start | bytes 25165828 | tf_op jit(solution)/shard_map/while
  273.1 5.2 copy-start.3
  273.1 6.5 copy-start.4
  288.9 12.4 %copy-start.2 = (f32[2048,1024]{1,0:T(8,128)S(1)}, f32[2048,1024]{1,0:T(8,128)}, u32[]{:S(2)}) copy-start(f32[2048,1024]{1,0:T(8,128)} %get-tuple-element.292) | copy-start | bytes 25165828 | tf_op jit(solution)/shard_map/while
  316.2 5.2 copy-start.3
  316.2 6.5 copy-start.4
  332.0 12.4 %copy-start.2 = (f32[2048,1024]{1,0:T(8,128)S(1)}, f32[2048,1024]{1,0:T(8,128)}, u32[]{:S(2)}) copy-start(f32[2048,1024]{1,0:T(8,128)} %get-tuple-element.292) | copy-start | bytes 25165828 | tf_op jit(solution)/shard_map/while
  359.2 5.2 copy-start.3
  359.3 6.5 copy-start.4
  375.0 12.4 %copy-start.2 = (f32[2048,1024]{1,0:T(8,128)S(1)}, f32[2048,1024]{1,0:T(8,128)}, u32[]{:S(2)}) copy-start(f32[2048,1024]{1,0:T(8,128)} %get-tuple-element.292) | copy-start | bytes 25165828 | tf_op jit(solution)/shard_map/while
  402.3 6.5 copy-start.4
  418.1 12.4 %copy-start.2 = (f32[2048,1024]{1,0:T(8,128)S(1)}, f32[2048,1024]{1,0:T(8,128)}, u32[]{:S(2)}) copy-start(f32[2048,1024]{1,0:T(8,128)} %get-tuple-element.292) | copy-start | bytes 25165828 | tf_op jit(solution)/shard_map/while
  445.4 6.5 copy-start.4
  461.1 12.4 %copy-start.2 = (f32[2048,1024]{1,0:T(8,128)S(1)}, f32[2048,1024]{1,0:T(8,128)}, u32[]{:S(2)}) copy-start(f32[2048,1024]{1,0:T(8,128)} %get-tuple-element.292) | copy-start | bytes 25165828 | tf_op jit(solution)/shard_map/while
  488.4 5.2 copy-start.3
  488.4 6.5 copy-start.4
  504.2 12.4 %copy-start.2 = (f32[2048,1024]{1,0:T(8,128)S(1)}, f32[2048,1024]{1,0:T(8,128)}, u32[]{:S(2)}) copy-start(f32[2048,1024]{1,0:T(8,128)} %get-tuple-element.292) | copy-start | bytes 25165828 | tf_op jit(solution)/shard_map/while
  531.5 5.2 copy-start.3
  531.5 6.5 copy-start.4
  547.3 12.4 %copy-start.2 = (f32[2048,1024]{1,0:T(8,128)S(1)}, f32[2048,1024]{1,0:T(8,128)}, u32[]{:S(2)}) copy-start(f32[2048,1024]{1,0:T(8,128)} %get-tuple-element.292) | copy-start | bytes 25165828 | tf_op jit(solution)/shard_map/while
  574.5 5.2 copy-start.3
  574.5 6.5 copy-start.4
  590.3 12.4 %copy-start.2 = (f32[2048,1024]{1,0:T(8,128)S(1)}, f32[2048,1024]{1,0:T(8,128)}, u32[]{:S(2)}) copy-start(f32[2048,1024]{1,0:T(8,128)} %get-tuple-element.292) | copy-start | bytes 25165828 | tf_op jit(solution)/shard_map/while
  617.6 5.2 copy-start.3
  617.6 6.5 copy-start.4
  633.4 12.4 %copy-start.2 = (f32[2048,1024]{1,0:T(8,128)S(1)}, f32[2048,1024]{1,0:T(8,128)}, u32[]{:S(2)}) copy-start(f32[2048,1024]{1,0:T(8,128)} %get-tuple-element.292) | copy-start | bytes 25165828 | tf_op jit(solution)/shard_map/while
  660.6 5.2 copy-start.3
  660.6 6.5 copy-start.4
  676.4 12.4 %copy-start.2 = (f32[2048,1024]{1,0:T(8,128)S(1)}, f32[2048,1024]{1,0:T(8,128)}, u32[]{:S(2)}) copy-start(f32[2048,1024]{1,0:T(8,128)} %get-tuple-element.292) | copy-start | bytes 25165828 | tf_op jit(solution)/shard_map/while
  703.7 5.2 copy-start.3
  703.7 6.5 copy-start.4
  719.5 12.4 %copy-start.2 = (f32[2048,1024]{1,0:T(8,128)S(1)}, f32[2048,1024]{1,0:T(8,128)}, u32[]{:S(2)}) copy-start(f32[2048,1024]{1,0:T(8,128)} %get-tuple-element.292) | copy-start | bytes 25165828 | tf_op jit(solution)/shard_map/while
  746.8 5.2 copy-start.3
  746.8 6.5 copy-start.4
  762.5 12.4 %copy-start.2 = (f32[2048,1024]{1,0:T(8,128)S(1)}, f32[2048,1024]{1,0:T(8,128)}, u32[]{:S(2)}) copy-start(f32[2048,1024]{1,0:T(8,128)} %get-tuple-element.292) | copy-start | bytes 25165828 | tf_op jit(solution)/shard_map/while
  789.8 5.2 copy-start.3
  789.8 6.5 copy-start.4
  805.6 12.4 %copy-start.2 = (f32[2048,1024]{1,0:T(8,128)S(1)}, f32[2048,1024]{1,0:T(8,128)}, u32[]{:S(2)}) copy-start(f32[2048,1024]{1,0:T(8,128)} %get-tuple-element.292) | copy-start | bytes 25165828 | tf_op jit(solution)/shard_map/while
  832.9 6.5 copy-start.4
  848.7 12.4 %copy-start.2 = (f32[2048,1024]{1,0:T(8,128)S(1)}, f32[2048,1024]{1,0:T(8,128)}, u32[]{:S(2)}) copy-start(f32[2048,1024]{1,0:T(8,128)} %get-tuple-element.292) | copy-start | bytes 25165828 | tf_op jit(solution)/shard_map/while
  875.9 6.5 copy-start.4
  891.7 12.4 %copy-start.2 = (f32[2048,1024]{1,0:T(8,128)S(1)}, f32[2048,1024]{1,0:T(8,128)}, u32[]{:S(2)}) copy-start(f32[2048,1024]{1,0:T(8,128)} %get-tuple-element.292) | copy-start | bytes 25165828 | tf_op jit(solution)/shard_map/while
  919.0 5.2 copy-start.3
  919.0 6.5 copy-start.4
  933.5 40.1 %copy-start.1 = (bf16[1024,192]{0,1:T(8,128)(2,1)S(1)}, bf16[1024,192]{0,1:T(8,128)(2,1)}, u32[]{:S(2)}) copy-start(bf16[1024,192]{0,1:T(8,128)(2,1)} %param.7) | copy-start | bytes 1179652
  (5 other events, 21.9 us)
Sparse Core Ops, SparseCore 0:
  13.2 178.8 all-gather.5
  221.9 26.6 all-gather.3
